TPU v7x, 32 devices: a whole 2x2x4 slice. The times are simulated.
32 devices in a mesh: dp: 8 (over z, core), tensor: 4 (over y, x).
Axes of the slice: x: 2, y: 2, z: 4, core: 2. Of those that a mesh axis runs over, the one named last changes fastest.
Arguments:
- tokens: bfloat16 [16, 512, 1024], P('dp', 'tensor'), may hold values from -8.5 to 8.5
- segment_ids: int32 [16, 512], P('dp'), may hold values from 0 to 5, never falling along the last dimension, each value on 1 to 128 neighbouring positions
- w_qkv: bfloat16 [3, 1024, 1024], P(None, 'dp', 'tensor'), may hold values from -0.2625 to 0.2625
- w_out: bfloat16 [1024, 1024], P('tensor', 'dp'), may hold values from -1.75 to 1.75
- w_up: bfloat16 [1024, 4096], P('dp', 'tensor'), may hold values from -0.1875 to 0.1875
- w_down: bfloat16 [4096, 1024], P('tensor', 'dp'), may hold values from -0.09375 to 0.09375
- vectors: bfloat16 [12, 1024], P(None, 'dp'), may hold values from -3 to 3
- cotangent: bfloat16 [16, 512, 1024], P('dp', 'tensor'), may hold values from -6 to 6
Outputs:
- out_tokens: bfloat16 [16, 512, 1024], P('dp', 'tensor')
- grad_tokens: float32 [16, 512, 1024], P('dp', 'tensor')
- grad_qkv: float32 [3, 1024, 1024], P(None, 'dp', 'tensor')
- grad_out: float32 [1024, 1024], P('tensor', 'dp')
- grad_up: float32 [1024, 4096], P('dp', 'tensor')
- grad_down: float32 [4096, 1024], P('tensor', 'dp')
- grad_vectors: float32 [12, 1024], P(None, 'dp')
Inputs may be any that keep to these rules, and one draw needn't show every extreme that they name: `segment_ids`: within a sequence the ids never fall; each document has 1 to 128 tokens and one has exactly that many.
All inputs are finite; a program needn't handle non-finite values.
Results may differ from a plain program's by a relative error of at most 0.02.
Values may be sent and summed in bfloat16 or wider, within the bound.
A program may use at most 128 MiB of HBM per device.

v0:
```python
import jax
import jax.numpy as jnp
from jax import lax
from jax.sharding import PartitionSpec as P

D = 1024
FF = 4096
HD = 64
NORM_EPS = 1e-06
SQRT_HALF = 0.7071067811865476
INV_ROOT_TAU = 0.3989422804014327
MASKED = -1e30


def gelu_value(pre_act):
    return 0.5 * pre_act * (1.0 + lax.erf(pre_act * SQRT_HALF))


def gelu_slope(pre_act):
    return 0.5 * (1.0 + lax.erf(pre_act * SQRT_HALF)) + pre_act * INV_ROOT_TAU * jnp.exp(
        -0.5 * pre_act * pre_act
    )


def norm_forward(summed, gain, shift):
    centred = summed - jnp.mean(summed, axis=-1, keepdims=True)
    inverse = lax.rsqrt(jnp.mean(centred * centred, axis=-1, keepdims=True) + NORM_EPS)
    normed = centred * inverse
    return (normed * gain + shift, normed, inverse)


def norm_backward(normed, inverse, grad_normed):
    first_mean = jnp.mean(grad_normed, axis=-1, keepdims=True)
    second_mean = jnp.mean(grad_normed * normed, axis=-1, keepdims=True)
    return inverse * (grad_normed - first_mean - normed * second_mean)


def attention_scores(query_heads, key_heads, segments):
    same_doc = segments[:, None] == segments[None, :]
    scores = jnp.einsum(
        "qhe,khe->hqk", query_heads, key_heads, preferred_element_type=jnp.float32
    ) * HD ** (-0.5)
    return jnp.where(same_doc[None], scores, MASKED)


def collect(w_qkv, w_out, w_up, w_down, vectors):
    return (
        lax.all_gather(w_qkv, "dp", axis=1, tiled=True),
        lax.all_gather(w_out, "dp", axis=1, tiled=True),
        lax.all_gather(w_up, "dp", axis=0, tiled=True),
        lax.all_gather(w_down, "dp", axis=1, tiled=True),
        lax.all_gather(vectors, "dp", axis=1, tiled=True),
    )


def share(gradients):
    return (
        lax.psum_scatter(
            gradients[0].astype(jnp.bfloat16), "dp", scatter_dimension=1, tiled=True
        ).astype(jnp.float32),
        lax.psum_scatter(
            gradients[1].astype(jnp.bfloat16), "dp", scatter_dimension=1, tiled=True
        ).astype(jnp.float32),
        lax.psum_scatter(
            gradients[2].astype(jnp.bfloat16), "dp", scatter_dimension=0, tiled=True
        ).astype(jnp.float32),
        lax.psum_scatter(
            gradients[3].astype(jnp.bfloat16), "dp", scatter_dimension=1, tiled=True
        ).astype(jnp.float32),
        lax.psum_scatter(
            gradients[4].astype(jnp.bfloat16), "dp", scatter_dimension=1, tiled=True
        ).astype(jnp.float32),
    )


def body(tokens, segment_ids, w_qkv, w_out, w_up, w_down, vectors, cotangent):
    tensor_rank = lax.axis_index("tensor")
    local_cols = w_qkv.shape[2]
    head_count = local_cols // HD
    hidden = w_up.shape[1]
    col_start = tensor_rank * local_cols
    ffn_start = tensor_rank * hidden

    def forward(weights, tok_block, segments):
        qkv_w, out_w, up_w, down_w, vec_b = weights
        vec_f32 = vec_b.astype(jnp.float32)
        whole = lax.all_gather(tok_block, "tensor", axis=0, tiled=True)
        seq_len = whole.shape[0]
        projected = jnp.einsum("sd,tdc->tsc", whole, qkv_w, preferred_element_type=jnp.float32)
        bias_q = lax.dynamic_slice_in_dim(vec_f32[0], col_start, local_cols)
        bias_v = lax.dynamic_slice_in_dim(vec_f32[1], col_start, local_cols)
        query_heads = (projected[0] + bias_q).astype(jnp.bfloat16).reshape(seq_len, head_count, HD)
        key_heads = projected[1].astype(jnp.bfloat16).reshape(seq_len, head_count, HD)
        value_heads = (projected[2] + bias_v).astype(jnp.bfloat16).reshape(seq_len, head_count, HD)
        scores = attention_scores(query_heads, key_heads, segments)
        row_top = jnp.max(scores, axis=-1, keepdims=True)
        log_total = row_top + jnp.log(jnp.sum(jnp.exp(scores - row_top), axis=-1, keepdims=True))
        attn_probs = jnp.exp(scores - log_total).astype(jnp.bfloat16)
        context = jnp.einsum(
            "hqk,khe->qhe", attn_probs, value_heads, preferred_element_type=jnp.float32
        )
        context = context.reshape(seq_len, local_cols).astype(jnp.bfloat16)
        piece = context
        attn_mixed = lax.psum_scatter(
            jnp.dot(piece, out_w, preferred_element_type=jnp.float32).astype(jnp.bfloat16),
            "tensor",
            scatter_dimension=0,
            tiled=True,
        ).astype(jnp.float32)
        summed_one = tok_block.astype(jnp.float32) + attn_mixed + vec_f32[2]
        normed_out, normed_one, inverse_one = norm_forward(summed_one, vec_f32[3], vec_f32[4])
        normed_b = normed_out.astype(jnp.bfloat16)
        normed_whole = lax.all_gather(normed_b, "tensor", axis=0, tiled=True)
        bias_up = lax.dynamic_slice_in_dim(vec_f32[8:12].reshape(FF), ffn_start, hidden)
        pre_act = jnp.dot(normed_whole, up_w, preferred_element_type=jnp.float32) + bias_up
        activated = gelu_value(pre_act).astype(jnp.bfloat16)
        piece = activated
        summed_two = (
            normed_out
            + lax.psum_scatter(
                jnp.dot(piece, down_w, preferred_element_type=jnp.float32).astype(jnp.bfloat16),
                "tensor",
                scatter_dimension=0,
                tiled=True,
            ).astype(jnp.float32)
            + vec_f32[5]
        )
        final, normed_two, inverse_two = norm_forward(summed_two, vec_f32[6], vec_f32[7])
        saved = (
            whole,
            query_heads,
            key_heads,
            value_heads,
            log_total,
            context,
            normed_one,
            inverse_one,
            normed_whole,
            pre_act,
            activated,
            normed_two,
            inverse_two,
        )
        return (final.astype(jnp.bfloat16), saved)

    def backward(weights, saved, segments, grad_block):
        qkv_w, out_w, up_w, down_w, vec_b = weights
        vec_f32 = vec_b.astype(jnp.float32)
        (
            whole,
            query_heads,
            key_heads,
            value_heads,
            log_total,
            context,
            normed_one,
            inverse_one,
            normed_whole,
            pre_act,
            activated,
            normed_two,
            inverse_two,
        ) = saved
        seq_len = whole.shape[0]
        grad_final = grad_block.astype(jnp.float32)
        g_gain2 = jnp.sum(grad_final * normed_two, axis=0)
        g_shift2 = jnp.sum(grad_final, axis=0)
        grad_two = norm_backward(normed_two, inverse_two, grad_final * vec_f32[6])
        grad_two_b = grad_two.astype(jnp.bfloat16)
        g_bdown = jnp.sum(grad_two, axis=0)
        grad_two_whole = lax.all_gather(grad_two_b, "tensor", axis=0, tiled=True)
        g_down = jnp.dot(activated.T, grad_two_whole, preferred_element_type=jnp.float32)
        grad_pre = jnp.dot(
            grad_two_whole, down_w.T, preferred_element_type=jnp.float32
        ) * gelu_slope(pre_act)
        grad_pre_b = grad_pre.astype(jnp.bfloat16)
        g_bup = jnp.sum(grad_pre, axis=0)
        g_up = jnp.dot(normed_whole.T, grad_pre_b, preferred_element_type=jnp.float32)
        piece = grad_pre_b
        grad_one_in = grad_two + lax.psum_scatter(
            jnp.dot(piece, up_w.T, preferred_element_type=jnp.float32).astype(jnp.bfloat16),
            "tensor",
            scatter_dimension=0,
            tiled=True,
        ).astype(jnp.float32)
        g_gain1 = jnp.sum(grad_one_in * normed_one, axis=0)
        g_shift1 = jnp.sum(grad_one_in, axis=0)
        grad_one = norm_backward(normed_one, inverse_one, grad_one_in * vec_f32[3])
        grad_one_b = grad_one.astype(jnp.bfloat16)
        g_bout = jnp.sum(grad_one, axis=0)
        grad_one_whole = lax.all_gather(grad_one_b, "tensor", axis=0, tiled=True)
        g_out = jnp.dot(context.T, grad_one_whole, preferred_element_type=jnp.float32)
        grad_context = jnp.dot(grad_one_whole, out_w.T, preferred_element_type=jnp.float32).astype(
            jnp.bfloat16
        )
        grad_context = grad_context.reshape(seq_len, head_count, HD)
        scores = attention_scores(query_heads, key_heads, segments)
        attn_exact = jnp.exp(scores - log_total)
        attn_probs = attn_exact.astype(jnp.bfloat16)
        grad_probs = jnp.einsum(
            "qhe,khe->hqk", grad_context, value_heads, preferred_element_type=jnp.float32
        )
        row_dot = jnp.sum(attn_exact * grad_probs, axis=-1, keepdims=True)
        grad_scores = (attn_exact * (grad_probs - row_dot) * HD ** (-0.5)).astype(jnp.bfloat16)
        grad_value = jnp.einsum(
            "hqk,qhe->khe", attn_probs, grad_context, preferred_element_type=jnp.float32
        )
        grad_value = grad_value.reshape(seq_len, local_cols)
        grad_query = jnp.einsum(
            "hqk,khe->qhe", grad_scores, key_heads, preferred_element_type=jnp.float32
        )
        grad_query = grad_query.reshape(seq_len, local_cols)
        grad_key = jnp.einsum(
            "hqk,qhe->khe", grad_scores, query_heads, preferred_element_type=jnp.float32
        )
        grad_key = grad_key.reshape(seq_len, local_cols)
        grad_qkv = jnp.stack([grad_query, grad_key, grad_value]).astype(jnp.bfloat16)
        g_qkv = jnp.einsum("sd,tsc->tdc", whole, grad_qkv, preferred_element_type=jnp.float32)
        piece = grad_qkv
        grad_input = grad_one + lax.psum_scatter(
            jnp.einsum("tsc,tdc->sd", piece, qkv_w, preferred_element_type=jnp.float32).astype(
                jnp.bfloat16
            ),
            "tensor",
            scatter_dimension=0,
            tiled=True,
        ).astype(jnp.float32)
        zero_row = jnp.zeros((D,), jnp.float32)
        row_q = lax.dynamic_update_slice_in_dim(zero_row, jnp.sum(grad_query, axis=0), col_start, 0)
        row_v = lax.dynamic_update_slice_in_dim(zero_row, jnp.sum(grad_value, axis=0), col_start, 0)
        up_rows = lax.dynamic_update_slice_in_dim(
            jnp.zeros((FF,), jnp.float32), g_bup, ffn_start, 0
        ).reshape(4, D)
        first_rows = jnp.stack(
            [row_q, row_v, g_bout, g_gain1, g_shift1, g_bdown, g_gain2, g_shift2]
        )
        g_vec = jnp.concatenate([first_rows, up_rows], axis=0)
        return ((g_qkv, g_out, g_up, g_down, g_vec), grad_input)

    def one_batch(carried, batch_item):
        tok_block, segments, grad_block = batch_item
        forward_w = collect(w_qkv, w_out, w_up, w_down, vectors)
        final_b, saved = forward(forward_w, tok_block, segments)
        second = collect(w_qkv, w_out, w_up, w_down, vectors)
        gradients, grad_input = backward(second, saved, segments, grad_block)
        updated = jax.tree.map(jnp.add, carried, gradients)
        return (updated, (final_b, grad_input))

    initial = (
        jnp.zeros((3, D, local_cols), jnp.float32),
        jnp.zeros((local_cols, D), jnp.float32),
        jnp.zeros((D, hidden), jnp.float32),
        jnp.zeros((hidden, D), jnp.float32),
        jnp.zeros((12, D), jnp.float32),
    )
    carried, stacked = lax.scan(one_batch, initial, (tokens, segment_ids, cotangent))
    totals = share(carried)
    vector_grads = lax.psum(totals[4], "tensor")
    return (stacked[0], stacked[1], totals[0], totals[1], totals[2], totals[3], vector_grads)


def solution(mesh):
    return jax.shard_map(
        body,
        mesh=mesh,
        in_specs=(
            P("dp", "tensor", None),
            P("dp", None),
            P(None, "dp", "tensor"),
            P("tensor", "dp"),
            P("dp", "tensor"),
            P("tensor", "dp"),
            P(None, "dp"),
            P("dp", "tensor", None),
        ),
        out_specs=(
            P("dp", "tensor", None),
            P("dp", "tensor", None),
            P(None, "dp", "tensor"),
            P("tensor", "dp"),
            P("dp", "tensor"),
            P("tensor", "dp"),
            P(None, "dp"),
        ),
        check_vma=False,
    )
```

profile of v0, /device:TPU:0, one launch (start us, length us, event | category | flops | bytes accessed | tf_op | source)
XLA Modules:
  0.0 942.0 jit_solution(16017847547988003658)
XLA Ops:
  9.8 748.5 %while.25 = (s32[]{:T(128)}, f32[3,1024,256]{1,2,0:T(8,128)}, f32[256,1024]{1,0:T(8,128)}, f32[1024,1024]{1,0:T(8,128)}, f32[1024,1024]{1,0:T(8,128)}, /*index=5...) while((s32[]{:T(128)}, f32[3,1024,256]{1,2,0:T(8,128)}, ...), condition=%wide.region_25.26_spmd.clone, body=%wide.region_0.25_spmd.clone.sunk | while | flops 10544906240 | bytes 269724672 | solution.py:256
  42.3 28.7 %all-gather.16.cloned.1.call-done = bf16[3,1024,256]{1,2,0:T(8,128)(2,1)} async-done(((bf16[3,128,256]{1,2,0:T(8,128)(2,1)}), bf16[3,1024,256]{1,2,0:T(8,128)(2,1)}) %all-gather.16.cloned.1.call-update) | async-done | bytes 1572880 | tf_op jit(solution)/shard_map/while/body/eval_jaxpr/all_gather | solution.py:48
  79.2 26.3 %reduce-scatter.26.cloned.1.call-done = bf16[128,1024]{1,0:T(8,128)(2,1)} async-done(((bf16[512,1024]{1,0:T(8,128)(2,1)}), bf16[128,1024]{1,0:T(8,128)(2,1)}) %reduce-scatter.26.cloned.1.call-update) | async-done | bytes 262160 | tf_op jit(solution)/shard_map/while/body/eval_jaxpr/reduce_scatter | solution.py:104
  110.3 25.8 %all-gather.20.cloned.1.call-done = bf16[1024,1024]{1,0:T(8,128)(2,1)} async-done(((bf16[128,1024]{1,0:T(8,128)(2,1)}), bf16[1024,1024]{1,0:T(8,128)(2,1)}) %all-gather.20.cloned.1.call-update) | async-done | bytes 2097168 | tf_op jit(solution)/shard_map/while/body/eval_jaxpr/all_gather | solution.py:50
  136.2 28.2 %all-gather.18.cloned.1.call-done = bf16[512,1024]{1,0:T(8,128)(2,1)} async-done(((bf16[128,1024]{1,0:T(8,128)(2,1)}), bf16[512,1024]{1,0:T(8,128)(2,1)}) %all-gather.18.cloned.1.call-update) | async-done | bytes 1048592 | tf_op jit(solution)/shard_map/while/body/eval_jaxpr/all_gather | solution.py:113
  168.9 27.5 %all-gather.14.cloned.1.call-done = bf16[1024,1024]{1,0:T(8,128)(2,1)} async-done(((bf16[1024,128]{1,0:T(8,128)(2,1)}), bf16[1024,1024]{1,0:T(8,128)(2,1)}) %all-gather.14.cloned.1.call-update) | async-done | bytes 2097168 | tf_op jit(solution)/shard_map/while/body/eval_jaxpr/all_gather | solution.py:51
  201.0 27.1 %reduce-scatter.28.cloned.1.call-done = bf16[128,1024]{1,0:T(8,128)(2,1)} async-done(((bf16[512,1024]{1,0:T(8,128)(2,1)}), bf16[128,1024]{1,0:T(8,128)(2,1)}) %reduce-scatter.28.cloned.1.call-update) | async-done | bytes 262160 | tf_op jit(solution)/shard_map/while/body/eval_jaxpr/reduce_scatter | solution.py:120
  232.4 26.6 %all-gather.22.cloned.1.call-done = bf16[512,1024]{1,0:T(8,128)(2,1)} async-done(((bf16[128,1024]{1,0:T(8,128)(2,1)}), bf16[512,1024]{1,0:T(8,128)(2,1)}) %all-gather.22.cloned.1.call-update) | async-done | bytes 1048592 | tf_op jit(solution)/shard_map/while/body/eval_jaxpr/all_gather | solution.py:171
  266.9 28.0 %reduce-scatter.30.cloned.1.call-done = bf16[128,1024]{1,0:T(8,128)(2,1)} async-done(((bf16[512,1024]{1,0:T(8,128)(2,1)}), bf16[128,1024]{1,0:T(8,128)(2,1)}) %reduce-scatter.30.cloned.1.call-update) | async-done | bytes 262160 | tf_op jit(solution)/shard_map/while/body/eval_jaxpr/reduce_scatter | solution.py:180
  303.1 23.9 %all-gather.24.cloned.1.call-done = bf16[512,1024]{1,0:T(8,128)(2,1)} async-done(((bf16[128,1024]{1,0:T(8,128)(2,1)}), bf16[512,1024]{1,0:T(8,128)(2,1)}) %all-gather.24.cloned.1.call-update) | async-done | bytes 1048592 | tf_op jit(solution)/shard_map/while/body/eval_jaxpr/all_gather | solution.py:191
  416.2 27.5 %all-gather.16.cloned.1.call-done = bf16[3,1024,256]{1,2,0:T(8,128)(2,1)} async-done(((bf16[3,128,256]{1,2,0:T(8,128)(2,1)}), bf16[3,1024,256]{1,2,0:T(8,128)(2,1)}) %all-gather.16.cloned.1.call-update) | async-done | bytes 1572880 | tf_op jit(solution)/shard_map/while/body/eval_jaxpr/all_gather | solution.py:48
  452.0 26.3 %reduce-scatter.26.cloned.1.call-done = bf16[128,1024]{1,0:T(8,128)(2,1)} async-done(((bf16[512,1024]{1,0:T(8,128)(2,1)}), bf16[128,1024]{1,0:T(8,128)(2,1)}) %reduce-scatter.26.cloned.1.call-update) | async-done | bytes 262160 | tf_op jit(solution)/shard_map/while/body/eval_jaxpr/reduce_scatter | solution.py:104
  483.1 25.8 %all-gather.20.cloned.1.call-done = bf16[1024,1024]{1,0:T(8,128)(2,1)} async-done(((bf16[128,1024]{1,0:T(8,128)(2,1)}), bf16[1024,1024]{1,0:T(8,128)(2,1)}) %all-gather.20.cloned.1.call-update) | async-done | bytes 2097168 | tf_op jit(solution)/shard_map/while/body/eval_jaxpr/all_gather | solution.py:50
  508.9 28.2 %all-gather.18.cloned.1.call-done = bf16[512,1024]{1,0:T(8,128)(2,1)} async-done(((bf16[128,1024]{1,0:T(8,128)(2,1)}), bf16[512,1024]{1,0:T(8,128)(2,1)}) %all-gather.18.cloned.1.call-update) | async-done | bytes 1048592 | tf_op jit(solution)/shard_map/while/body/eval_jaxpr/all_gather | solution.py:113
  541.6 27.5 %all-gather.14.cloned.1.call-done = bf16[1024,1024]{1,0:T(8,128)(2,1)} async-done(((bf16[1024,128]{1,0:T(8,128)(2,1)}), bf16[1024,1024]{1,0:T(8,128)(2,1)}) %all-gather.14.cloned.1.call-update) | async-done | bytes 2097168 | tf_op jit(solution)/shard_map/while/body/eval_jaxpr/all_gather | solution.py:51
  573.7 27.1 %reduce-scatter.28.cloned.1.call-done = bf16[128,1024]{1,0:T(8,128)(2,1)} async-done(((bf16[512,1024]{1,0:T(8,128)(2,1)}), bf16[128,1024]{1,0:T(8,128)(2,1)}) %reduce-scatter.28.cloned.1.call-update) | async-done | bytes 262160 | tf_op jit(solution)/shard_map/while/body/eval_jaxpr/reduce_scatter | solution.py:120
  605.0 26.6 %all-gather.22.cloned.1.call-done = bf16[512,1024]{1,0:T(8,128)(2,1)} async-done(((bf16[128,1024]{1,0:T(8,128)(2,1)}), bf16[512,1024]{1,0:T(8,128)(2,1)}) %all-gather.22.cloned.1.call-update) | async-done | bytes 1048592 | tf_op jit(solution)/shard_map/while/body/eval_jaxpr/all_gather | solution.py:171
  639.6 28.0 %reduce-scatter.30.cloned.1.call-done = bf16[128,1024]{1,0:T(8,128)(2,1)} async-done(((bf16[512,1024]{1,0:T(8,128)(2,1)}), bf16[128,1024]{1,0:T(8,128)(2,1)}) %reduce-scatter.30.cloned.1.call-update) | async-done | bytes 262160 | tf_op jit(solution)/shard_map/while/body/eval_jaxpr/reduce_scatter | solution.py:180
  675.8 23.9 %all-gather.24.cloned.1.call-done = bf16[512,1024]{1,0:T(8,128)(2,1)} async-done(((bf16[128,1024]{1,0:T(8,128)(2,1)}), bf16[512,1024]{1,0:T(8,128)(2,1)}) %all-gather.24.cloned.1.call-update) | async-done | bytes 1048592 | tf_op jit(solution)/shard_map/while/body/eval_jaxpr/all_gather | solution.py:191
  774.5 17.9 %reduce-scatter.24.cloned.1.call-done = bf16[128,12]{1,0:T(8,128)(2,1)} async-done(((bf16[1024,12]{1,0:T(8,128)(2,1)}), bf16[128,12]{1,0:T(8,128)(2,1)}) %reduce-scatter.24.cloned.1.call-update) | async-done | bytes 3088
  803.8 20.7 %reduce-scatter.20.cloned.1.call-done = bf16[128,256]{1,0:T(8,128)(2,1)} async-done(((bf16[1024,256]{1,0:T(8,128)(2,1)}), bf16[128,256]{1,0:T(8,128)(2,1)}) %reduce-scatter.20.cloned.1.call-update) | async-done | bytes 65552
  826.1 32.9 %reduce-scatter.16.cloned.1.call-done = bf16[3,128,256]{2,1,0:T(8,128)(2,1)} async-done(((bf16[3,1024,256]{2,1,0:T(8,128)(2,1)}), bf16[3,128,256]{2,1,0:T(8,128)(2,1)}) %reduce-scatter.16.cloned.1.call-update) | async-done | bytes 196624 | tf_op jit(solution)/shard_map/reduce_scatter | solution.py:58
  860.7 35.1 %reduce-scatter.22.cloned.1.call-done = bf16[128,1024]{1,0:T(8,128)(2,1)} async-done(((bf16[1024,1024]{1,0:T(8,128)(2,1)}), bf16[128,1024]{1,0:T(8,128)(2,1)}) %reduce-scatter.22.cloned.1.call-update) | async-done | bytes 262160
  897.7 34.9 %reduce-scatter.18.cloned.1.call-done = bf16[128,1024]{1,0:T(8,128)(2,1)} async-done(((bf16[1024,1024]{1,0:T(8,128)(2,1)}), bf16[128,1024]{1,0:T(8,128)(2,1)}) %reduce-scatter.18.cloned.1.call-update) | async-done | bytes 262160 | tf_op jit(solution)/shard_map/reduce_scatter | solution.py:64
  (326 shorter events, 300.8 us)
Async XLA Ops:
  11.5 59.5 %all-gather.16.cloned.1.call-start = ((), (), s32[]{:S(2)}) async-start(), calls=%async_computation.16 | async-start | bytes 1769472 | tf_op jit(solution)/shard_map/while/body/eval_jaxpr/all_gather | solution.py:48
  12.3 93.2 %reduce-scatter.26.cloned.1.call-start = ((), (), s32[]{:S(2)}) async-start(), calls=%async_computation.17 | async-start | bytes 1310720 | tf_op jit(solution)/shard_map/while/body/eval_jaxpr/reduce_scatter | solution.py:104
  78.6 57.6 %all-gather.20.cloned.1.call-start = ((), (), s32[]{:S(2)}) async-start(), calls=%async_computation.19 | async-start | bytes 2359296 | tf_op jit(solution)/shard_map/while/body/eval_jaxpr/all_gather | solution.py:50
  79.2 85.2 %all-gather.18.cloned.1.call-start = ((), (), s32[]{:S(2)}) async-start(), calls=%async_computation.18 | async-start | bytes 1310720 | tf_op jit(solution)/shard_map/while/body/eval_jaxpr/all_gather | solution.py:113
  109.7 86.8 %all-gather.14.cloned.1.call-start = ((), (), s32[]{:S(2)}) async-start(), calls=%async_computation.15 | async-start | bytes 2359296 | tf_op jit(solution)/shard_map/while/body/eval_jaxpr/all_gather | solution.py:51
  110.2 117.9 %reduce-scatter.28.cloned.1.call-start = ((), (), s32[]{:S(2)}) async-start(), calls=%async_computation.20 | async-start | bytes 1310720 | tf_op jit(solution)/shard_map/while/body/eval_jaxpr/reduce_scatter | solution.py:120
  201.0 58.0 %all-gather.22.cloned.1.call-start = ((), (), s32[]{:S(2)}) async-start(), calls=%async_computation.21 | async-start | bytes 1310720 | tf_op jit(solution)/shard_map/while/body/eval_jaxpr/all_gather | solution.py:171
  232.3 62.6 %reduce-scatter.30.cloned.1.call-start = ((), (), s32[]{:S(2)}) async-start(), calls=%async_computation.22 | async-start | bytes 1310720 | tf_op jit(solution)/shard_map/while/body/eval_jaxpr/reduce_scatter | solution.py:180
  266.9 60.0 %all-gather.24.cloned.1.call-start = ((), (), s32[]{:S(2)}) async-start(), calls=%async_computation.23 | async-start | bytes 1310720 | tf_op jit(solution)/shard_map/while/body/eval_jaxpr/all_gather | solution.py:191
  300.3 83.3 %reduce-scatter.32.cloned.1.call-start = ((), (), s32[]{:S(2)}) async-start(), calls=%async_computation.24 | async-start | bytes 1310720 | tf_op jit(solution)/shard_map/while/body/eval_jaxpr/reduce_scatter | solution.py:220
  387.3 56.4 %all-gather.16.cloned.1.call-start = ((), (), s32[]{:S(2)}) async-start(), calls=%async_computation.16 | async-start | bytes 1769472 | tf_op jit(solution)/shard_map/while/body/eval_jaxpr/all_gather | solution.py:48
  388.0 90.2 %reduce-scatter.26.cloned.1.call-start = ((), (), s32[]{:S(2)}) async-start(), calls=%async_computation.17 | async-start | bytes 1310720 | tf_op jit(solution)/shard_map/while/body/eval_jaxpr/reduce_scatter | solution.py:104
  451.3 57.5 %all-gather.20.cloned.1.call-start = ((), (), s32[]{:S(2)}) async-start(), calls=%async_computation.19 | async-start | bytes 2359296 | tf_op jit(solution)/shard_map/while/body/eval_jaxpr/all_gather | solution.py:50
  451.9 85.1 %all-gather.18.cloned.1.call-start = ((), (), s32[]{:S(2)}) async-start(), calls=%async_computation.18 | async-start | bytes 1310720 | tf_op jit(solution)/shard_map/while/body/eval_jaxpr/all_gather | solution.py:113
  482.4 86.8 %all-gather.14.cloned.1.call-start = ((), (), s32[]{:S(2)}) async-start(), calls=%async_computation.15 | async-start | bytes 2359296 | tf_op jit(solution)/shard_map/while/body/eval_jaxpr/all_gather | solution.py:51
  483.0 117.8 %reduce-scatter.28.cloned.1.call-start = ((), (), s32[]{:S(2)}) async-start(), calls=%async_computation.20 | async-start | bytes 1310720 | tf_op jit(solution)/shard_map/while/body/eval_jaxpr/reduce_scatter | solution.py:120
  573.7 58.0 %all-gather.22.cloned.1.call-start = ((), (), s32[]{:S(2)}) async-start(), calls=%async_computation.21 | async-start | bytes 1310720 | tf_op jit(solution)/shard_map/while/body/eval_jaxpr/all_gather | solution.py:171
  605.0 62.6 %reduce-scatter.30.cloned.1.call-start = ((), (), s32[]{:S(2)}) async-start(), calls=%async_computation.22 | async-start | bytes 1310720 | tf_op jit(solution)/shard_map/while/body/eval_jaxpr/reduce_scatter | solution.py:180
  639.6 60.0 %all-gather.24.cloned.1.call-start = ((), (), s32[]{:S(2)}) async-start(), calls=%async_computation.23 | async-start | bytes 1310720 | tf_op jit(solution)/shard_map/while/body/eval_jaxpr/all_gather | solution.py:191
  673.0 83.4 %reduce-scatter.32.cloned.1.call-start = ((), (), s32[]{:S(2)}) async-start(), calls=%async_computation.24 | async-start | bytes 1310720 | tf_op jit(solution)/shard_map/while/body/eval_jaxpr/reduce_scatter | solution.py:220
  759.3 65.2 %reduce-scatter.20.cloned.1.call-start = ((), (), s32[]{:S(2)}) async-start(), calls=%async_computation.11 | async-start | bytes 589824
  763.5 95.5 %reduce-scatter.16.cloned.1.call-start = ((), (), s32[]{:S(2)}) async-start(), calls=%async_computation.9 | async-start | bytes 1769472 | tf_op jit(solution)/shard_map/reduce_scatter | solution.py:58
  765.3 130.5 %reduce-scatter.22.cloned.1.call-start = ((), (), s32[]{:S(2)}) async-start(), calls=%async_computation.12 | async-start | bytes 2359296
  770.5 162.1 %reduce-scatter.18.cloned.1.call-start = ((), (), s32[]{:S(2)}) async-start(), calls=%async_computation.10 | async-start | bytes 2359296 | tf_op jit(solution)/shard_map/reduce_scatter | solution.py:64
  (58 other events, 1026.5 us)
Sparse Core Ops, SparseCore 0:
  13.0 29.2 all-gather.11
  43.9 27.0 all-gather.15
  78.7 26.7 reduce-scatter.25
  107.0 29.1 all-gather.19
  138.4 25.8 all-gather.17
  165.8 30.5 all-gather.13
  201.1 26.9 reduce-scatter.27
  232.4 26.4 all-gather.21
  267.0 27.9 reduce-scatter.29
  300.4 26.4 all-gather.23
  355.6 27.9 reduce-scatter.31
  388.5 26.4 all-gather.11
  416.6 27.0 all-gather.15
  451.4 26.7 reduce-scatter.25
  479.7 29.1 all-gather.19
  511.1 25.8 all-gather.17
  538.5 30.5 all-gather.13
  573.8 26.9 reduce-scatter.27
  605.1 26.4 all-gather.21
  639.7 27.9 reduce-scatter.29
  673.1 26.4 all-gather.23
  728.3 27.9 reduce-scatter.31
Sparse Core Ops, SparseCore 1:
  761.6 30.7 reduce-scatter.23
  795.1 29.4 reduce-scatter.19
  826.7 32.3 reduce-scatter.15
  861.3 34.4 reduce-scatter.21
  898.1 34.4 reduce-scatter.17
where the time goes:
time: 944 us; the launch traced here: 942 us
  waiting for transfers between devices  649 us (69%)
  matrix products  131 us (14%)
  blocking collectives  66.2 us (7%)
  other arithmetic  50.2 us (5%)
  local copies, waits for them, and re-layouts  27.1 us (3%)
  between operations  15.8 us (2%)
    unnamed x8, waiting for transfers between devices  73.8 us
    all_gather x2, waiting for transfers between devices, forward(): normed_whole = lax.all_gather(normed_b, 'tensor', axis=0, tiled=True)  56.4 us
    all_gather x2, waiting for transfers between devices, collect(): lax.all_gather(w_qkv, 'dp', axis=1, tiled=True)  56.2 us
    reduce_scatter x2, waiting for transfers between devices, backward(): lax.psum_scatter(jnp.dot(piece, up_w.T, preferred_element_type=jnp.float3...  56.1 us
    all_gather x2, waiting for transfers between devices, collect(): lax.all_gather(w_down, 'dp', axis=1, tiled=True)  55.1 us
    reduce_scatter x2, waiting for transfers between devices, forward(): lax.psum_scatter(jnp.dot(piece, down_w, preferred_element_type=jnp.float3...  54.1 us
    all_gather x2, waiting for transfers between devices, backward(): grad_two_whole = lax.all_gather(grad_two_b, 'tensor', axis=0, tiled=True)  53.2 us
    reduce_scatter x2, waiting for transfers between devices, forward(): lax.psum_scatter(jnp.dot(piece, out_w, preferred_element_type=jnp.float32...  52.5 us
  transfers between devices with their start and end apart: 27, of which 26 were waited for; matrix products, arithmetic and copies ran while one was open for 8% of the time, Pallas kernels for 0%

commit v1 on v0

--- a/solution.py
+++ b/solution.py
@@ -1,3 +1,4 @@
+import functools
 import jax
 import jax.numpy as jnp
 from jax import lax
@@ -12,6 +13,21 @@
 MASKED = -1e30
 
 
+def plan_map(u_in, join_dim):
+    y, placed, taken_in = (lax.axis_size("dp"), lax.axis_index("dp"), u_in.shape[join_dim])
+    block_list = [src_i * y if k == join_dim else src_i for k, src_i in enumerate(u_in.shape)]
+    z1 = lax.dynamic_update_slice_in_dim(
+        jnp.zeros(block_list, u_in.dtype), u_in, placed * taken_in, axis=join_dim
+    )
+    for i in [*range(1, y)]:
+        u_in = lax.ppermute(u_in, "dp", perm=[(k, (k + 1) % y) for k in range(y)])
+        z1 = lax.dynamic_update_slice_in_dim(z1, u_in, (placed - i) % y * taken_in, axis=join_dim)
+    return z1
+
+
+_edit_sample = functools.partial(plan_map, join_dim=1)
+
+
 def gelu_value(pre_act):
     return 0.5 * pre_act * (1.0 + lax.erf(pre_act * SQRT_HALF))
 
@@ -45,7 +61,7 @@
 
 def collect(w_qkv, w_out, w_up, w_down, vectors):
     return (
-        lax.all_gather(w_qkv, "dp", axis=1, tiled=True),
+        _edit_sample(w_qkv),
         lax.all_gather(w_out, "dp", axis=1, tiled=True),
         lax.all_gather(w_up, "dp", axis=0, tiled=True),
         lax.all_gather(w_down, "dp", axis=1, tiled=True),

time: 944 us -> 893 us (0.946)
  waiting for transfers between devices: 649 us -> 586 us
  local copies, waits for them, and re-layouts: 27.1 us -> 40.6 us
    all_gather x2 -> x0, waiting for transfers between devices: 56.2 us -> none  [collect(): lax.all_gather(w_qkv, 'dp', axis=1, tiled=True)]
    all_gather x2, waiting for transfers between devices: 51.6 us -> 0.05 us  [collect(): lax.all_gather(w_up, 'dp', axis=0, tiled=True)]
    ppermute x0 -> x7, waiting for transfers between devices: none -> 50.9 us  [plan_map(): u_in = lax.ppermute(u_in, 'dp', perm=[(k, (k + 1) % y) for k in range(y)])]
    dynamic_update_slice x0 -> x16, local copies, waits for them, and re-layouts: none -> 15.2 us  [the longest x14 13.3 us: plan_map(): lax.dynamic_update_slice_in_dim(z1, u_in, (placed - i) % y * taken_in, ax...]
  transfers between devices with their start and end apart: 27 -> 32, of which waited for: 26 -> 28; matrix products, arithmetic and copies ran while one was open for 8% -> 11% of each run, Pallas kernels for 0% -> 0%
where the time goes in v1:
time: 893 us; the launch traced here: 891 us
  waiting for transfers between devices  586 us (66%)
  matrix products  131 us (15%)
  blocking collectives  64.6 us (7%)
  other arithmetic  50.3 us (6%)
  local copies, waits for them, and re-layouts  40.6 us (5%)
  between operations  15.7 us (2%)
    unnamed x8, waiting for transfers between devices  73.9 us
    reduce_scatter x2, waiting for transfers between devices, backward(): lax.psum_scatter(jnp.dot(piece, up_w.T, preferred_element_type=jnp.float3...  56.1 us
    all_gather x2, waiting for transfers between devices, collect(): lax.all_gather(w_down, 'dp', axis=1, tiled=True)  54.7 us
    reduce_scatter x2, waiting for transfers between devices, forward(): lax.psum_scatter(jnp.dot(piece, down_w, preferred_element_type=jnp.float3...  53.9 us
    all_gather x2, waiting for transfers between devices, backward(): grad_two_whole = lax.all_gather(grad_two_b, 'tensor', axis=0, tiled=True)  53.2 us
    all_gather x2, waiting for transfers between devices, forward(): normed_whole = lax.all_gather(normed_b, 'tensor', axis=0, tiled=True)  53 us
    reduce_scatter x2, waiting for transfers between devices, forward(): lax.psum_scatter(jnp.dot(piece, out_w, preferred_element_type=jnp.float32...  51.2 us
    ppermute x7, waiting for transfers between devices, plan_map(): u_in = lax.ppermute(u_in, 'dp', perm=[(k, (k + 1) % y) for k in range(y)])  50.9 us
  transfers between devices with their start and end apart: 32, of which 28 were waited for; matrix products, arithmetic and copies ran while one was open for 11% of the time, Pallas kernels for 0%

profile of v1, /device:TPU:0, one launch (start us, length us, event | category | flops | bytes accessed | tf_op | source)
XLA Modules:
  0.0 891.5 jit_solution(3127280565707347597)
XLA Ops:
  59.5 648.3 %while.25 = (s32[]{:T(128)}, f32[3,1024,256]{1,2,0:T(8,128)}, f32[256,1024]{1,0:T(8,128)}, f32[1024,1024]{1,0:T(8,128)}, f32[1024,1024]{1,0:T(8,128)}, /*index=5...) while((s32[]{:T(128)}, f32[3,1024,256]{1,2,0:T(8,128)}, ...), condition=%wide.region_25.26_spmd.clone, body=%wide.region_0.25_spmd.clone.sunk | while | flops 10544906240 | bytes 277787072 | solution.py:272
  83.1 14.3 %all_gather.68 = bf16[256,1024]{1,0:T(8,128)(2,1)S(1)} all-gather(bf16[256,128]{1,0:T(8,128)(2,1)S(1)} %copy-done.23), channel_id=1, replica_groups=mesh['dp'=8,'tensor'=4] {'dp'}, dimensions={1}, use_global_device_ids=true | all-gather | bytes 589824 | tf_op jit(solution)/shard_map/while/body/eval_jaxpr/all_gather | solution.py:65
  105.4 26.3 %reduce-scatter.26.cloned.1.call-done = bf16[128,1024]{1,0:T(8,128)(2,1)} async-done(((bf16[512,1024]{1,0:T(8,128)(2,1)}), bf16[128,1024]{1,0:T(8,128)(2,1)}) %reduce-scatter.26.cloned.1.call-update) | async-done | bytes 262160 | tf_op jit(solution)/shard_map/while/body/eval_jaxpr/reduce_scatter | solution.py:120
  136.5 26.3 %all-gather.15.cloned.1.call-done = bf16[512,1024]{1,0:T(8,128)(2,1)} async-done(((bf16[128,1024]{1,0:T(8,128)(2,1)}), bf16[512,1024]{1,0:T(8,128)(2,1)}) %all-gather.15.cloned.1.call-update) | async-done | bytes 1048592 | tf_op jit(solution)/shard_map/while/body/eval_jaxpr/all_gather | solution.py:129
  167.4 27.4 %all-gather.13.cloned.1.call-done = bf16[1024,1024]{1,0:T(8,128)(2,1)} async-done(((bf16[1024,128]{1,0:T(8,128)(2,1)}), bf16[1024,1024]{1,0:T(8,128)(2,1)}) %all-gather.13.cloned.1.call-update) | async-done | bytes 2097168 | tf_op jit(solution)/shard_map/while/body/eval_jaxpr/all_gather | solution.py:67
  199.3 27.0 %reduce-scatter.28.cloned.1.call-done = bf16[128,1024]{1,0:T(8,128)(2,1)} async-done(((bf16[512,1024]{1,0:T(8,128)(2,1)}), bf16[128,1024]{1,0:T(8,128)(2,1)}) %reduce-scatter.28.cloned.1.call-update) | async-done | bytes 262160 | tf_op jit(solution)/shard_map/while/body/eval_jaxpr/reduce_scatter | solution.py:136
  230.6 26.6 %all-gather.19.cloned.1.call-done = bf16[512,1024]{1,0:T(8,128)(2,1)} async-done(((bf16[128,1024]{1,0:T(8,128)(2,1)}), bf16[512,1024]{1,0:T(8,128)(2,1)}) %all-gather.19.cloned.1.call-update) | async-done | bytes 1048592 | tf_op jit(solution)/shard_map/while/body/eval_jaxpr/all_gather | solution.py:187
  265.2 28.0 %reduce-scatter.30.cloned.1.call-done = bf16[128,1024]{1,0:T(8,128)(2,1)} async-done(((bf16[512,1024]{1,0:T(8,128)(2,1)}), bf16[128,1024]{1,0:T(8,128)(2,1)}) %reduce-scatter.30.cloned.1.call-update) | async-done | bytes 262160 | tf_op jit(solution)/shard_map/while/body/eval_jaxpr/reduce_scatter | solution.py:196
  301.2 23.8 %all-gather.21.cloned.1.call-done = bf16[512,1024]{1,0:T(8,128)(2,1)} async-done(((bf16[128,1024]{1,0:T(8,128)(2,1)}), bf16[512,1024]{1,0:T(8,128)(2,1)}) %all-gather.21.cloned.1.call-update) | async-done | bytes 1048592 | tf_op jit(solution)/shard_map/while/body/eval_jaxpr/all_gather | solution.py:207
  369.3 13.0 %reduce-scatter.32.cloned.1.call-done = bf16[128,1024]{1,0:T(8,128)(2,1)} async-done(((bf16[512,1024]{1,0:T(8,128)(2,1)}), bf16[128,1024]{1,0:T(8,128)(2,1)}) %reduce-scatter.32.cloned.1.call-update) | async-done | bytes 262160 | tf_op jit(solution)/shard_map/while/body/eval_jaxpr/reduce_scatter | solution.py:236
  386.1 13.0 %all_gather.66 = bf16[12,1024]{1,0:T(8,128)(2,1)S(1)} all-gather(bf16[12,128]{1,0:T(8,128)(2,1)} %get-tuple-element.780), channel_id=1, replica_groups=mesh['dp'=8,'tensor'=4] {'dp'}, dimensions={1}, use_global_device_ids=true | all-gather | bytes 27648 | tf_op jit(solution)/shard_map/while/body/eval_jaxpr/all_gather | solution.py:68
  407.9 13.7 %all_gather.68 = bf16[256,1024]{1,0:T(8,128)(2,1)S(1)} all-gather(bf16[256,128]{1,0:T(8,128)(2,1)S(1)} %copy-done.23), channel_id=1, replica_groups=mesh['dp'=8,'tensor'=4] {'dp'}, dimensions={1}, use_global_device_ids=true | all-gather | bytes 589824 | tf_op jit(solution)/shard_map/while/body/eval_jaxpr/all_gather | solution.py:65
  429.8 24.9 %reduce-scatter.26.cloned.1.call-done = bf16[128,1024]{1,0:T(8,128)(2,1)} async-done(((bf16[512,1024]{1,0:T(8,128)(2,1)}), bf16[128,1024]{1,0:T(8,128)(2,1)}) %reduce-scatter.26.cloned.1.call-update) | async-done | bytes 262160 | tf_op jit(solution)/shard_map/while/body/eval_jaxpr/reduce_scatter | solution.py:120
  459.6 26.7 %all-gather.15.cloned.1.call-done = bf16[512,1024]{1,0:T(8,128)(2,1)} async-done(((bf16[128,1024]{1,0:T(8,128)(2,1)}), bf16[512,1024]{1,0:T(8,128)(2,1)}) %all-gather.15.cloned.1.call-update) | async-done | bytes 1048592 | tf_op jit(solution)/shard_map/while/body/eval_jaxpr/all_gather | solution.py:129
  490.9 27.4 %all-gather.13.cloned.1.call-done = bf16[1024,1024]{1,0:T(8,128)(2,1)} async-done(((bf16[1024,128]{1,0:T(8,128)(2,1)}), bf16[1024,1024]{1,0:T(8,128)(2,1)}) %all-gather.13.cloned.1.call-update) | async-done | bytes 2097168 | tf_op jit(solution)/shard_map/while/body/eval_jaxpr/all_gather | solution.py:67
  522.8 27.0 %reduce-scatter.28.cloned.1.call-done = bf16[128,1024]{1,0:T(8,128)(2,1)} async-done(((bf16[512,1024]{1,0:T(8,128)(2,1)}), bf16[128,1024]{1,0:T(8,128)(2,1)}) %reduce-scatter.28.cloned.1.call-update) | async-done | bytes 262160 | tf_op jit(solution)/shard_map/while/body/eval_jaxpr/reduce_scatter | solution.py:136
  554.1 26.6 %all-gather.19.cloned.1.call-done = bf16[512,1024]{1,0:T(8,128)(2,1)} async-done(((bf16[128,1024]{1,0:T(8,128)(2,1)}), bf16[512,1024]{1,0:T(8,128)(2,1)}) %all-gather.19.cloned.1.call-update) | async-done | bytes 1048592 | tf_op jit(solution)/shard_map/while/body/eval_jaxpr/all_gather | solution.py:187
  588.6 28.0 %reduce-scatter.30.cloned.1.call-done = bf16[128,1024]{1,0:T(8,128)(2,1)} async-done(((bf16[512,1024]{1,0:T(8,128)(2,1)}), bf16[128,1024]{1,0:T(8,128)(2,1)}) %reduce-scatter.30.cloned.1.call-update) | async-done | bytes 262160 | tf_op jit(solution)/shard_map/while/body/eval_jaxpr/reduce_scatter | solution.py:196
  624.7 23.8 %all-gather.21.cloned.1.call-done = bf16[512,1024]{1,0:T(8,128)(2,1)} async-done(((bf16[128,1024]{1,0:T(8,128)(2,1)}), bf16[512,1024]{1,0:T(8,128)(2,1)}) %all-gather.21.cloned.1.call-update) | async-done | bytes 1048592 | tf_op jit(solution)/shard_map/while/body/eval_jaxpr/all_gather | solution.py:207
  724.0 17.9 %reduce-scatter.24.cloned.1.call-done = bf16[128,12]{1,0:T(8,128)(2,1)} async-done(((bf16[1024,12]{1,0:T(8,128)(2,1)}), bf16[128,12]{1,0:T(8,128)(2,1)}) %reduce-scatter.24.cloned.1.call-update) | async-done | bytes 3088
  753.3 20.9 %reduce-scatter.20.cloned.1.call-done = bf16[128,256]{1,0:T(8,128)(2,1)} async-done(((bf16[1024,256]{1,0:T(8,128)(2,1)}), bf16[128,256]{1,0:T(8,128)(2,1)}) %reduce-scatter.20.cloned.1.call-update) | async-done | bytes 65552
  775.8 32.9 %reduce-scatter.16.cloned.1.call-done = bf16[3,128,256]{2,1,0:T(8,128)(2,1)} async-done(((bf16[3,1024,256]{2,1,0:T(8,128)(2,1)}), bf16[3,128,256]{2,1,0:T(8,128)(2,1)}) %reduce-scatter.16.cloned.1.call-update) | async-done | bytes 196624 | tf_op jit(solution)/shard_map/reduce_scatter | solution.py:74
  810.4 35.1 %reduce-scatter.22.cloned.1.call-done = bf16[128,1024]{1,0:T(8,128)(2,1)} async-done(((bf16[1024,1024]{1,0:T(8,128)(2,1)}), bf16[128,1024]{1,0:T(8,128)(2,1)}) %reduce-scatter.22.cloned.1.call-update) | async-done | bytes 262160
  847.5 34.6 %reduce-scatter.18.cloned.1.call-done = bf16[128,1024]{1,0:T(8,128)(2,1)} async-done(((bf16[1024,1024]{1,0:T(8,128)(2,1)}), bf16[128,1024]{1,0:T(8,128)(2,1)}) %reduce-scatter.18.cloned.1.call-update) | async-done | bytes 262160 | tf_op jit(solution)/shard_map/reduce_scatter | solution.py:80
  (367 shorter events, 309.1 us)
Async XLA Ops:
  59.5 38.1 %all-gather.11.cloned.1.call-start = ((), (), s32[]{:S(2)}) async-start(), calls=%async_computation.14 | async-start | bytes 1310720 | tf_op jit(solution)/shard_map/while/body/eval_jaxpr/all_gather | solution.py:103
  61.2 70.4 %reduce-scatter.26.cloned.1.call-start = ((), (), s32[]{:S(2)}) async-start(), calls=%async_computation.16 | async-start | bytes 1310720 | tf_op jit(solution)/shard_map/while/body/eval_jaxpr/reduce_scatter | solution.py:120
  104.7 31.8 %all-gather.17.cloned.1.call-start = ((), (), s32[]{:S(2)}) async-start(), calls=%async_computation.18 | async-start | bytes 2359296 | tf_op jit(solution)/shard_map/while/body/eval_jaxpr/all_gather | solution.py:66
  105.3 57.5 %all-gather.15.cloned.1.call-start = ((), (), s32[]{:S(2)}) async-start(), calls=%async_computation.17 | async-start | bytes 1310720 | tf_op jit(solution)/shard_map/while/body/eval_jaxpr/all_gather | solution.py:129
  135.8 58.9 %all-gather.13.cloned.1.call-start = ((), (), s32[]{:S(2)}) async-start(), calls=%async_computation.15 | async-start | bytes 2359296 | tf_op jit(solution)/shard_map/while/body/eval_jaxpr/all_gather | solution.py:67
  136.4 89.9 %reduce-scatter.28.cloned.1.call-start = ((), (), s32[]{:S(2)}) async-start(), calls=%async_computation.19 | async-start | bytes 1310720 | tf_op jit(solution)/shard_map/while/body/eval_jaxpr/reduce_scatter | solution.py:136
  199.3 57.9 %all-gather.19.cloned.1.call-start = ((), (), s32[]{:S(2)}) async-start(), calls=%async_computation.20 | async-start | bytes 1310720 | tf_op jit(solution)/shard_map/while/body/eval_jaxpr/all_gather | solution.py:187
  230.5 62.7 %reduce-scatter.30.cloned.1.call-start = ((), (), s32[]{:S(2)}) async-start(), calls=%async_computation.21 | async-start | bytes 1310720 | tf_op jit(solution)/shard_map/while/body/eval_jaxpr/reduce_scatter | solution.py:196
  265.1 59.9 %all-gather.21.cloned.1.call-start = ((), (), s32[]{:S(2)}) async-start(), calls=%async_computation.22 | async-start | bytes 1310720 | tf_op jit(solution)/shard_map/while/body/eval_jaxpr/all_gather | solution.py:207
  298.5 83.9 %reduce-scatter.32.cloned.1.call-start = ((), (), s32[]{:S(2)}) async-start(), calls=%async_computation.23 | async-start | bytes 1310720 | tf_op jit(solution)/shard_map/while/body/eval_jaxpr/reduce_scatter | solution.py:236
  384.3 37.6 %all-gather.11.cloned.1.call-start = ((), (), s32[]{:S(2)}) async-start(), calls=%async_computation.14 | async-start | bytes 1310720 | tf_op jit(solution)/shard_map/while/body/eval_jaxpr/all_gather | solution.py:103
  386.1 68.6 %reduce-scatter.26.cloned.1.call-start = ((), (), s32[]{:S(2)}) async-start(), calls=%async_computation.16 | async-start | bytes 1310720 | tf_op jit(solution)/shard_map/while/body/eval_jaxpr/reduce_scatter | solution.py:120
  429.8 56.5 %all-gather.15.cloned.1.call-start = ((), (), s32[]{:S(2)}) async-start(), calls=%async_computation.17 | async-start | bytes 1310720 | tf_op jit(solution)/shard_map/while/body/eval_jaxpr/all_gather | solution.py:129
  458.8 59.4 %all-gather.13.cloned.1.call-start = ((), (), s32[]{:S(2)}) async-start(), calls=%async_computation.15 | async-start | bytes 2359296 | tf_op jit(solution)/shard_map/while/body/eval_jaxpr/all_gather | solution.py:67
  459.4 90.4 %reduce-scatter.28.cloned.1.call-start = ((), (), s32[]{:S(2)}) async-start(), calls=%async_computation.19 | async-start | bytes 1310720 | tf_op jit(solution)/shard_map/while/body/eval_jaxpr/reduce_scatter | solution.py:136
  522.8 57.9 %all-gather.19.cloned.1.call-start = ((), (), s32[]{:S(2)}) async-start(), calls=%async_computation.20 | async-start | bytes 1310720 | tf_op jit(solution)/shard_map/while/body/eval_jaxpr/all_gather | solution.py:187
  554.0 62.7 %reduce-scatter.30.cloned.1.call-start = ((), (), s32[]{:S(2)}) async-start(), calls=%async_computation.21 | async-start | bytes 1310720 | tf_op jit(solution)/shard_map/while/body/eval_jaxpr/reduce_scatter | solution.py:196
  588.6 59.9 %all-gather.21.cloned.1.call-start = ((), (), s32[]{:S(2)}) async-start(), calls=%async_computation.22 | async-start | bytes 1310720 | tf_op jit(solution)/shard_map/while/body/eval_jaxpr/all_gather | solution.py:207
  622.0 83.9 %reduce-scatter.32.cloned.1.call-start = ((), (), s32[]{:S(2)}) async-start(), calls=%async_computation.23 | async-start | bytes 1310720 | tf_op jit(solution)/shard_map/while/body/eval_jaxpr/reduce_scatter | solution.py:236
  707.8 34.0 %reduce-scatter.24.cloned.1.call-start = ((), (), s32[]{:S(2)}) async-start(), calls=%async_computation.13 | async-start | bytes 294912
  708.8 65.4 %reduce-scatter.20.cloned.1.call-start = ((), (), s32[]{:S(2)}) async-start(), calls=%async_computation.11 | async-start | bytes 589824
  713.0 95.7 %reduce-scatter.16.cloned.1.call-start = ((), (), s32[]{:S(2)}) async-start(), calls=%async_computation.9 | async-start | bytes 1769472 | tf_op jit(solution)/shard_map/reduce_scatter | solution.py:74
  714.8 130.7 %reduce-scatter.22.cloned.1.call-start = ((), (), s32[]{:S(2)}) async-start(), calls=%async_computation.12 | async-start | bytes 2359296
  720.0 162.1 %reduce-scatter.18.cloned.1.call-start = ((), (), s32[]{:S(2)}) async-start(), calls=%async_computation.10 | async-start | bytes 2359296 | tf_op jit(solution)/shard_map/reduce_scatter | solution.py:80
  (71 other events, 825.7 us)
Sparse Core Ops, SparseCore 0:
  62.7 25.1 all-gather.10
  104.8 26.7 reduce-scatter.25
  199.4 26.8 reduce-scatter.27
  230.7 26.4 all-gather.18
  265.2 27.9 reduce-scatter.29
  354.4 27.9 reduce-scatter.31
  387.5 26.4 all-gather.10
  429.1 25.5 reduce-scatter.25
  522.9 26.8 reduce-scatter.27
  554.1 26.4 all-gather.18
  588.7 27.9 reduce-scatter.29
  677.9 27.9 reduce-scatter.31
Sparse Core Ops, SparseCore 1:
  106.8 27.9 all-gather.16
  137.1 25.7 all-gather.14
  164.3 30.4 all-gather.12
  298.6 26.3 all-gather.20
  431.4 26.6 all-gather.16
  460.6 25.7 all-gather.14
  487.8 30.4 all-gather.12
  622.1 26.3 all-gather.20
  711.1 30.7 reduce-scatter.23
  744.7 29.4 reduce-scatter.19
  776.4 32.3 reduce-scatter.15
  811.1 34.4 reduce-scatter.21
  847.7 34.4 reduce-scatter.17
